TPU v7x, 32 devices: a whole 2x2x4 slice. The times are simulated.
32 devices in a mesh: dp: 4 (over z), expert: 4 (over y, x), tensor: 2 (over core).
Axes of the slice: x: 2, y: 2, z: 4, core: 2. Of those that a mesh axis runs over, the one named last changes fastest.
Arguments:
- tokens: bfloat16 [512, 6144], P('dp', 'tensor'), may hold values from -6 to 6
- out_grad: bfloat16 [512, 6144], P('dp', 'tensor'), may hold values from -6 to 6
- router_weight: bfloat16 [6144, 4], P('tensor'), may hold values from -0.078125 to 0.078125
- gate_weight: bfloat16 [4, 6144, 8192], P('expert', 'tensor', 'dp'), may hold values from -0.078125 to 0.078125
- up_weight: bfloat16 [4, 6144, 8192], P('expert', 'tensor', 'dp'), may hold values from -0.078125 to 0.078125
- down_weight: bfloat16 [4, 8192, 6144], P('expert', 'dp', 'tensor'), may hold values from -0.0625 to 0.0625
- expert_index: int32 [512, 2], P('dp'), may hold values from 0 to 3, as said below
- slot_index: int32 [512, 2], P('dp'), may hold values from 0 to 95, as said below
Outputs:
- tokens_grad: bfloat16 [512, 6144], P(('dp', 'expert'), 'tensor')
- router_grad: float32 [6144, 4], P('tensor')
- gate_grad: bfloat16 [4, 6144, 8192], P('expert', 'tensor', 'dp')
- up_grad: bfloat16 [4, 6144, 8192], P('expert', 'tensor', 'dp')
- down_grad: bfloat16 [4, 8192, 6144], P('expert', 'dp', 'tensor')
Inputs may be any that keep to these rules, and one draw needn't show every extreme that they name: `expert_index`: each row names two different experts; in each aligned block of 128 rows no expert is named more than 96 times, and one expert is named exactly 96 times in every block. `slot_index`: entry k of a row is a slot of the expert in entry k of the same row of expert_index; within one aligned block of 128 rows the choices of one expert have distinct slots.
All inputs are finite; a program needn't handle non-finite values.
Results may differ from a plain program's by a relative error of at most 0.025.
Values may be sent and summed in bfloat16 or wider, within the bound.
A program may use at most 128 MiB of HBM per device.

v0:
```python
import jax
import jax.numpy as jnp
from jax import lax
from jax.sharding import PartitionSpec as P

CAP = 96
highest = lax.Precision.HIGHEST


def contract_rows(left_side, right_side):
    return lax.dot_general(
        left_side, right_side, (((0,), (0,)), ((), ())), preferred_element_type=jnp.float32
    )


def contract_cols(left_side, right_side):
    return lax.dot_general(
        left_side, right_side, (((1,), (1,)), ((), ())), preferred_element_type=jnp.float32
    )


def split_parts(values):
    high_part = values.astype(jnp.bfloat16)
    low_part = (values - high_part.astype(jnp.float32)).astype(jnp.bfloat16)
    return (high_part, low_part)


def table_apply(form, table_low, values):
    high_part, low_part = split_parts(values)
    return jnp.einsum(form, table_low, high_part, preferred_element_type=jnp.float32) + jnp.einsum(
        form, table_low, low_part, preferred_element_type=jnp.float32
    )


def slot_table(experts_here, slots_here, expert_id, capacity):
    positions = lax.broadcasted_iota(jnp.int32, (capacity, experts_here.shape[0]), 0)
    first_table = (experts_here[:, 0] == expert_id)[None, :] & (
        slots_here[:, 0][None, :] == positions
    )
    second_table = (experts_here[:, 1] == expert_id)[None, :] & (
        slots_here[:, 1][None, :] == positions
    )
    return (first_table.astype(jnp.float32), second_table.astype(jnp.float32))


def hidden_terms(gate_sum, up_sum, grad_act, slot_prob):
    gate_sigmoid = jax.nn.sigmoid(gate_sum)
    hidden = (gate_sum * gate_sigmoid * up_sum).astype(jnp.bfloat16)
    prob_grad = jnp.sum(hidden.astype(jnp.float32) * grad_act, axis=1)
    act_grad = slot_prob.astype(jnp.float32)[:, None] * grad_act
    grad_gate = (act_grad * up_sum * gate_sigmoid * (1.0 + gate_sum * (1.0 - gate_sigmoid))).astype(
        jnp.bfloat16
    )
    grad_up = (act_grad * gate_sum * gate_sigmoid).astype(jnp.bfloat16)
    return (hidden, grad_gate, grad_up, prob_grad)


def shards(
    tokens, out_grad, router_weight, gate_weight, up_weight, down_weight, expert_index, slot_index
):
    capacity = CAP
    expert_count = router_weight.shape[1]
    expert_id = lax.axis_index("expert")
    logits = lax.psum(jnp.dot(tokens, router_weight, preferred_element_type=jnp.float32), "tensor")
    chosen = jnp.take_along_axis(logits, expert_index, axis=1)
    pick_prob = jnp.stack(
        [jax.nn.sigmoid(chosen[:, 0] - chosen[:, 1]), jax.nn.sigmoid(chosen[:, 1] - chosen[:, 0])],
        axis=1,
    )
    prob_wide = pick_prob.astype(jnp.bfloat16).astype(jnp.float32)
    first_table, second_table = slot_table(expert_index, slot_index, expert_id, capacity)
    select = first_table + second_table
    select_low = select.astype(jnp.bfloat16)
    local_tokens = jnp.dot(select_low, tokens, preferred_element_type=jnp.float32).astype(
        jnp.bfloat16
    )
    local_grads = jnp.dot(select_low, out_grad, preferred_element_type=jnp.float32).astype(
        jnp.bfloat16
    )
    local_prob = (
        jnp.dot(first_table, prob_wide[:, 0], precision=highest)
        + jnp.dot(second_table, prob_wide[:, 1], precision=highest)
    ).astype(jnp.bfloat16)
    slot_tokens, slot_grads, slot_prob = (
        lax.all_gather(local_tokens, "dp", axis=0, tiled=True),
        lax.all_gather(local_grads, "dp", axis=0, tiled=True),
        lax.all_gather(local_prob, "dp", axis=0, tiled=True),
    )
    gate_block = gate_weight[0]
    up_block = up_weight[0]
    down_block = down_weight[0]
    gate_part = jnp.dot(slot_tokens, gate_block, preferred_element_type=jnp.float32)
    up_part = jnp.dot(slot_tokens, up_block, preferred_element_type=jnp.float32)
    grad_part = contract_cols(slot_grads, down_block)
    gate_sum, up_sum, grad_sum = (
        lax.psum(gate_part.astype(jnp.bfloat16), "tensor").astype(jnp.float32),
        lax.psum(up_part.astype(jnp.bfloat16), "tensor").astype(jnp.float32),
        lax.psum(grad_part.astype(jnp.bfloat16), "tensor").astype(jnp.float32),
    )
    hidden, grad_gate, grad_up, prob_grad = hidden_terms(gate_sum, up_sum, grad_sum, slot_prob)
    scaled_grads = (slot_prob.astype(jnp.float32)[:, None] * slot_grads.astype(jnp.float32)).astype(
        jnp.bfloat16
    )
    down_grad = contract_rows(hidden, scaled_grads).astype(jnp.bfloat16)
    gate_grad = contract_rows(slot_tokens, grad_gate).astype(jnp.bfloat16)
    up_grad = contract_rows(slot_tokens, grad_up).astype(jnp.bfloat16)
    slot_dx = contract_cols(grad_gate, gate_block) + contract_cols(grad_up, up_block)
    own_expert = (lax.broadcasted_iota(jnp.int32, (1, expert_count), 1) == expert_id).astype(
        jnp.float32
    )
    row_dx, row_prob = (
        lax.psum_scatter(
            slot_dx.astype(jnp.bfloat16), "dp", scatter_dimension=0, tiled=True
        ).astype(jnp.float32),
        lax.psum_scatter(
            prob_grad.astype(jnp.bfloat16), "dp", scatter_dimension=0, tiled=True
        ).astype(jnp.float32),
    )
    token_dx = table_apply("cn,cd->nd", select_low, row_dx)
    token_prob = table_apply("cn,c->n", select_low, row_prob)
    token_term, prob_rows = (
        lax.psum_scatter(
            token_dx.astype(jnp.bfloat16), "expert", scatter_dimension=0, tiled=True
        ).astype(jnp.float32),
        lax.psum_scatter(
            (token_prob[:, None] * own_expert).astype(jnp.bfloat16),
            "expert",
            scatter_dimension=0,
            tiled=True,
        ).astype(jnp.float32),
    )
    quarter = token_term.shape[0]
    offset = expert_id * quarter
    part_prob = lax.dynamic_slice_in_dim(pick_prob, offset, quarter, 0)
    part_experts = lax.dynamic_slice_in_dim(expert_index, offset, quarter, 0)
    part_tokens = lax.dynamic_slice_in_dim(tokens, offset, quarter, 0)
    pick_grad = jnp.take_along_axis(prob_rows, part_experts, axis=1)
    mixed_grad = jnp.sum(part_prob * pick_grad, axis=1, keepdims=True)
    weights = part_prob * (pick_grad - mixed_grad)
    onehot = (
        part_experts[:, :, None] == lax.broadcasted_iota(jnp.int32, (1, 1, expert_count), 2)
    ).astype(jnp.float32)
    logit_grad = jnp.sum(onehot * weights[:, :, None], axis=1)
    router_rows = router_weight.astype(jnp.float32)
    tokens_grad = (token_term + jnp.dot(logit_grad, router_rows.T, precision=highest)).astype(
        jnp.bfloat16
    )
    router_part = jnp.dot(part_tokens.astype(jnp.float32).T, logit_grad, precision=highest)
    router_grad = lax.psum(router_part, ("dp", "expert"))
    return (tokens_grad, router_grad, gate_grad[None], up_grad[None], down_grad[None])


def solution(mesh):
    in_specs = (
        P("dp", "tensor"),
        P("dp", "tensor"),
        P("tensor", None),
        P("expert", "tensor", "dp"),
        P("expert", "tensor", "dp"),
        P("expert", "dp", "tensor"),
        P("dp", None),
        P("dp", None),
    )
    out_specs = (
        P(("dp", "expert"), "tensor"),
        P("tensor", None),
        P("expert", "tensor", "dp"),
        P("expert", "tensor", "dp"),
        P("expert", "dp", "tensor"),
    )
    return jax.shard_map(shards, mesh=mesh, in_specs=in_specs, out_specs=out_specs, check_vma=False)
```

profile of v0, /device:TPU:0, one launch (start us, length us, event | category | flops | bytes accessed | tf_op | source)
XLA Modules:
  0.0 356.0 jit_solution(7405413484927864889)
XLA Ops:
  7.2 0.8 slice_bitcast_fusion.1
  8.0 0.8 compare_bitcast_fusion.1
  8.8 1.1 convolution_convert_fusion
  10.0 2.3 convolution_convert_fusion.1
  12.3 50.6 %all-gather.5.cloned.1.call-done = bf16[384,3072]{1,0:T(8,128)(2,1)} async-done(((bf16[96,3072]{1,0:T(8,128)(2,1)}), bf16[384,3072]{1,0:T(8,128)(2,1)}) %all-gather.5.cloned.1.call-update) | async-done | bytes 2359312 | tf_op jit(solution)/shard_map/all_gather | solution.py:85
  62.9 11.3 %fusion.31 = bf16[384,2048]{1,0:T(8,128)(2,1)} fusion(bf16[384,3072]{1,0:T(8,128)(2,1)} %all-gather.5.cloned.1.call-done, bf16[1,3072,2048]{2,1,0:T(8,128)(2,1)} %param.11), kind=kOutput, calls=%fused_computation.44 | convolution fusion | flops 4832624640 | bytes 16515072 | tf_op jit(solution)/shard_map/dot_general | solution.py:92
  74.1 9.4 %fusion.28 = bf16[384,2048]{1,0:T(8,128)(2,1)} fusion(bf16[384,3072]{1,0:T(8,128)(2,1)S(1)} %copy-done.8, bf16[1,3072,2048]{2,1,0:T(8,128)(2,1)} %param.12), kind=kOutput, calls=%fused_computation.43 | convolution fusion | flops 4832624640 | bytes 16515072 | tf_op jit(solution)/shard_map/dot_general | solution.py:93
  83.5 30.3 %all-gather.3.cloned.1.call-done = bf16[384,3072]{1,0:T(8,128)(2,1)} async-done(((bf16[96,3072]{1,0:T(8,128)(2,1)}), bf16[384,3072]{1,0:T(8,128)(2,1)}) %all-gather.3.cloned.1.call-update) | async-done | bytes 2359312 | tf_op jit(solution)/shard_map/all_gather | solution.py:86
  113.8 9.6 %fusion.25 = bf16[384,2048]{1,0:T(8,128)(2,1)} fusion(bf16[384,3072]{1,0:T(8,128)(2,1)} %all-gather.3.cloned.1.call-done, bf16[1,2048,3072]{2,1,0:T(8,128)(2,1)} %param.13), kind=kOutput, calls=%fused_computation.42 | convolution fusion | flops 4832624640 | bytes 16515072 | tf_op jit(solution)/shard_map/dot_general | solution.py:17
  123.5 0.6 copy-done.6
  124.4 0.3 fusion.66
  124.7 2.5 psum.35
  127.2 2.4 gather_fusion
  129.7 0.6 fusion.65
  131.5 20.0 %all-reduce.6.cloned.1.call-done = (bf16[384,2048]{1,0:T(8,128)(2,1)}, bf16[384,2048]{1,0:T(8,128)(2,1)}, bf16[384,2048]{1,0:T(8,128)(2,1)}) async-done(((bf16[384,2048]{1,0:T(8,128)(2,1)}, bf16[384,2048]{1,0:T(8,128)(2,1)}, bf16[384,2048]{1,0:T(8,128)(2,1)}), (bf16[384,2048]{1,0:T(8,128)(2,1)}, bf16[384,2048]{1,0:T(8,128)(2,1)}, bf16[384,2048]{1,0:T(8,128)(2,1)})) %all-reduce.6.cloned.1.call-update) | async-done | bytes 4718608 | tf_op jit(solution)/shard_map/psum | solution.py:98
  151.5 3.7 %fusion.14 = bf16[384]{0:T(512)(128)(2,1)S(1)} fusion(bf16[384,2048]{1,0:T(8,128)(2,1)} %get-tuple-element.7, bf16[384,2048]{1,0:T(8,128)(2,1)} %get-tuple-element.8, bf16[384,2048]{1,0:T(8,128)(2,1)} %get-tuple-element.9), kind=kLoop, calls=%fused_computation.31 | loop fusion | flops 9436800 | bytes 4719360 | tf_op jit(solution)/shard_map/reduce_sum | solution.py:49
  155.2 12.1 %all-reduce.2 = (bf16[384]{0:T(512)(128)(2,1)S(1)}, bf16[384]{0:T(512)(128)(2,1)S(1)}) all-reduce(bf16[384]{0:T(512)(128)(2,1)S(1)} %fusion.14, bf16[384]{0:T(512)(128)(2,1)S(1)} %dynamic-update-slice), channel_id=4, replica_groups=mesh['dp'=4,'expert'=4,'tensor'=2] {'dp'}, use_global_device_ids=true, to_apply=%region_7.8.clone | all-reduce | flops 768 | bytes 3072
  167.4 12.2 %fusion = f32[384,3072]{1,0:T(8,128)} fusion(bf16[1,3072,2048]{2,1,0:T(8,128)(2,1)} %param.11, bf16[384,2048]{1,0:T(8,128)(2,1)S(1)} %copy-done.1, bf16[384,2048]{1,0:T(8,128)(2,1)} %get-tuple-element.7, bf16[384,2048]{1,0:T(8,128)(2,1)} %get-tuple-element.9, f32[384]{0:T(512)S(1)} %convert_element_type.124), kind=kOutput, calls=%fused_computation.2 | convolution fusion | flops 4842848256 | bytes 22021632 | tf_op jit(solution)/shard_map/dot_general | solution.py:17
  179.6 16.1 %add_convert_fusion = bf16[384,3072]{1,0:T(8,128)(2,1)} fusion(f32[384,3072]{1,0:T(8,128)} %fusion, bf16[1,3072,2048]{2,1,0:T(8,128)(2,1)} %param.12, bf16[384,2048]{1,0:T(8,128)(2,1)S(1)} %copy-done.2, bf16[384,2048]{1,0:T(8,128)(2,1)} %get-tuple-element.7, f32[384]{0:T(512)S(1)} %convert_element_type.124), kind=kOutput, calls=%fused_computation.20 | convolution fusion | flops 4841275392 | bytes 22808064 | tf_op jit(solution)/shard_map/dot_general | solution.py:17
  197.2 0.7 copy.63
  198.0 0.3 reduce-scatter.8.cloned.1.call-start
  198.3 13.5 %convert_bitcast_fusion.2 = bf16[1,3072,2048]{2,1,0:T(8,128)(2,1)} fusion(bf16[384,3072]{1,0:T(8,128)(2,1)} %all-gather.5.cloned.1.call-done, bf16[384,2048]{1,0:T(8,128)(2,1)S(1)} %copy-done.1, bf16[384,2048]{1,0:T(8,128)(2,1)} %get-tuple-element.7, bf16[384,2048]{1,0:T(8,128)(2,1)} %get-tuple-element.9, f32[384]{0:T(512)S(1)} %convert_element_type.124), kind=kOutput, calls=%fused_computation.14 | convolution fusion | flops 4849139712 | bytes 19662336 | tf_op jit(solution)/shard_map/dot_general | solution.py:11
  211.8 10.3 %convert_bitcast_fusion.1 = bf16[1,3072,2048]{2,1,0:T(8,128)(2,1)} fusion(bf16[384,3072]{1,0:T(8,128)(2,1)S(1)} %copy-done.9, bf16[384,2048]{1,0:T(8,128)(2,1)S(1)} %copy-done.3, bf16[384,2048]{1,0:T(8,128)(2,1)S(1)} %copy-done.4, f32[384]{0:T(512)S(1)} %convert_element_type.124), kind=kOutput, calls=%fused_computation.13 | convolution fusion | flops 4845207552 | bytes 18089472 | tf_op jit(solution)/shard_map/dot_general | solution.py:11
  222.1 19.6 %reduce-scatter.6.cloned.1.call-done = bf16[96,3072]{1,0:T(8,128)(2,1)} async-done(((bf16[384,3072]{1,0:T(8,128)(2,1)}), bf16[96,3072]{1,0:T(8,128)(2,1)}) %reduce-scatter.6.cloned.1.call-update) | async-done | bytes 589840 | tf_op jit(solution)/shard_map/reduce_scatter | solution.py:112
  241.8 1.5 fusion.48
  243.2 2.4 fusion.12
  245.6 12.1 %convert_bitcast_fusion = bf16[1,2048,3072]{2,1,0:T(8,128)(2,1)} fusion(bf16[384,3072]{1,0:T(8,128)(2,1)} %all-gather.3.cloned.1.call-done, f32[384]{0:T(512)S(1)} %convert_element_type.124, bf16[384,2048]{1,0:T(8,128)(2,1)S(1)} %copy-done.1, bf16[384,2048]{1,0:T(8,128)(2,1)} %get-tuple-element.9), kind=kOutput, calls=%fused_computation.12 | convolution fusion | flops 4847960064 | bytes 18089472 | tf_op jit(solution)/shard_map/dot_general | solution.py:11
  257.7 10.6 %reduce-scatter.10.cloned.1.call-done = bf16[32,4]{1,0:T(8,128)(2,1)} async-done(((bf16[128,4]{1,0:T(8,128)(2,1)}), bf16[32,4]{1,0:T(8,128)(2,1)}) %reduce-scatter.10.cloned.1.call-update) | async-done | bytes 272
  268.4 0.8 copy.64
  269.2 0.9 gather_fusion.1
  270.6 76.5 %psum.39 = f32[3072,4]{0,1:T(4,128)} all-reduce(f32[3072,4]{0,1:T(4,128)S(1)} %fusion.38), channel_id=1, replica_groups=mesh['dp'=4,'expert'=4,'tensor'=2] {'dp','expert'}, use_global_device_ids=true, to_apply=%region_11.12 | all-reduce | flops 12288 | bytes 98304 | tf_op jit(solution)/shard_map/psum | solution.py:149
  347.1 2.0 fusion.13
  (59 shorter events, 2.6 us)
Async XLA Ops:
  7.2 1.6 copy-start
  7.2 55.7 %all-gather.5.cloned.1.call-start = ((), (), s32[]{:S(2)}) async-start(), calls=%async_computation.4 | async-start | bytes 2949120 | tf_op jit(solution)/shard_map/all_gather | solution.py:85
  9.9 103.9 %all-gather.3.cloned.1.call-start = ((), (), s32[]{:S(2)}) async-start(), calls=%async_computation.3 | async-start | bytes 2949120 | tf_op jit(solution)/shard_map/all_gather | solution.py:86
  12.3 139.3 %all-reduce.6.cloned.1.call-start = ((), (), s32[]{:S(2)}) async-start(), calls=%async_computation.8 | async-start | bytes 9437184 | tf_op jit(solution)/shard_map/psum | solution.py:98
  62.9 11.3 %copy-start.8 = (bf16[384,3072]{1,0:T(8,128)(2,1)S(1)}, bf16[384,3072]{1,0:T(8,128)(2,1)}, u32[]{:S(2)}) copy-start(bf16[384,3072]{1,0:T(8,128)(2,1)} %all-gather.5.cloned.1.call-done) | copy-start | bytes 7077892
  123.4 0.7 copy-start.6
  123.4 0.9 copy-start.5
  123.5 118.3 %reduce-scatter.6.cloned.1.call-start = ((), (), s32[]{:S(2)}) async-start(), calls=%async_computation.5 | async-start | bytes 2949120 | tf_op jit(solution)/shard_map/reduce_scatter | solution.py:112
  127.2 2.6 copy-start.7
  151.5 15.8 %copy-start.1 = (bf16[384,2048]{1,0:T(8,128)(2,1)S(1)}, bf16[384,2048]{1,0:T(8,128)(2,1)}, u32[]{:S(2)}) copy-start(bf16[384,2048]{1,0:T(8,128)(2,1)} %get-tuple-element.8) | copy-start | bytes 4718596
  167.4 12.2 %copy-start.2 = (bf16[384,2048]{1,0:T(8,128)(2,1)S(1)}, bf16[384,2048]{1,0:T(8,128)(2,1)}, u32[]{:S(2)}) copy-start(bf16[384,2048]{1,0:T(8,128)(2,1)} %get-tuple-element.9) | copy-start | bytes 4718596
  195.7 72.6 %reduce-scatter.10.cloned.1.call-start = ((), (), s32[]{:S(2)}) async-start(), calls=%async_computation.7 | async-start | bytes 40960
  198.0 149.2 %reduce-scatter.8.cloned.1.call-start = ((), (), s32[]{:S(2)}) async-start(), calls=%async_computation.6 | async-start | bytes 983040 | tf_op jit(solution)/shard_map/reduce_scatter | solution.py:122
  198.2 13.5 %copy-start.3 = (bf16[384,2048]{1,0:T(8,128)(2,1)S(1)}, bf16[384,2048]{1,0:T(8,128)(2,1)}, u32[]{:S(2)}) copy-start(bf16[384,2048]{1,0:T(8,128)(2,1)} %get-tuple-element.9) | copy-start | bytes 4718596
  198.3 13.5 %copy-start.4 = (bf16[384,2048]{1,0:T(8,128)(2,1)S(1)}, bf16[384,2048]{1,0:T(8,128)(2,1)}, u32[]{:S(2)}) copy-start(bf16[384,2048]{1,0:T(8,128)(2,1)} %get-tuple-element.7) | copy-start | bytes 4718596
  198.3 13.5 %copy-start.9 = (bf16[384,3072]{1,0:T(8,128)(2,1)S(1)}, bf16[384,3072]{1,0:T(8,128)(2,1)}, u32[]{:S(2)}) copy-start(bf16[384,3072]{1,0:T(8,128)(2,1)} %all-gather.5.cloned.1.call-done) | copy-start | bytes 7077892
Sparse Core Ops, SparseCore 0:
  10.1 52.6 all-gather.4
  65.0 48.7 all-gather.2
  123.6 27.9 all-reduce.5
  195.9 45.8 reduce-scatter.5
  244.9 23.4 reduce-scatter.9
  271.1 26.3 reduce-scatter.7
where the time goes:
time: 356 us
  waiting for transfers between devices  131 us (37%)
  matrix products  105 us (29%)
  blocking collectives  91.1 us (26%)
  between operations  15.6 us (4%)
  local copies, waits for them, and re-layouts  7.8 us (2%)
  other arithmetic  4.83 us (1%)
    psum x1, blocking collectives, shards(): router_grad = lax.psum(router_part, ('dp', 'expert'))  76.5 us
    all_gather x1, waiting for transfers between devices, shards(): lax.all_gather(local_tokens, 'dp', axis=0, tiled=True)  50.6 us
    dot_general x3, matrix products, contract_cols(): lax.dot_general(left_side, right_side, (((1,), (1,)), ((), ())), preferre...  38 us
    dot_general x3, matrix products, contract_rows(): lax.dot_general(left_side, right_side, (((0,), (0,)), ((), ())), preferre...  36 us
    all_gather x1, waiting for transfers between devices, shards(): lax.all_gather(local_grads, 'dp', axis=0, tiled=True)  30.3 us
    psum x1, waiting for transfers between devices, shards(): lax.psum(grad_part.astype(jnp.bfloat16), 'tensor').astype(jnp.float32)  20 us
    reduce_scatter x1, waiting for transfers between devices, shards(): lax.psum_scatter(slot_dx.astype(jnp.bfloat16), 'dp', scatter_dimension=0,...  19.6 us
    unnamed x1, blocking collectives  12.1 us
  transfers between devices with their start and end apart: 6, of which 5 were waited for; matrix products, arithmetic and copies ran while one was open for 20% of the time, Pallas kernels for 0%

commit v1 on v0

--- a/solution.py
+++ b/solution.py
@@ -146,7 +146,7 @@
         jnp.bfloat16
     )
     router_part = jnp.dot(part_tokens.astype(jnp.float32).T, logit_grad, precision=highest)
-    router_grad = lax.psum(router_part, ("dp", "expert"))
+    router_grad = jnp.sum(lax.all_gather(router_part, ("dp", "expert")), axis=0)
     return (tokens_grad, router_grad, gate_grad[None], up_grad[None], down_grad[None])
 
 

time: 356 us -> 326 us (0.916)
  blocking collectives: 91.1 us -> 59.5 us
    psum x1 -> x0, blocking collectives: 76.5 us -> none  [shards(): router_grad = lax.psum(router_part, ('dp', 'expert'))]
    all_gather x0 -> x1, blocking collectives: none -> 44.9 us  [shards(): router_grad = jnp.sum(lax.all_gather(router_part, ('dp', 'expert')), axis=0)]
  transfers between devices with their start and end apart: 6 -> 6, of which waited for: 5 -> 5; matrix products, arithmetic and copies ran while one was open for 20% -> 22% of each run, Pallas kernels for 0% -> 0%
where the time goes in v1:
time: 326 us; the launch traced here: 325 us
  waiting for transfers between devices  131 us (40%)
  matrix products  105 us (32%)
  blocking collectives  59.5 us (18%)
  between operations  15.6 us (5%)
  local copies, waits for them, and re-layouts  7.8 us (2%)
  other arithmetic  5.97 us (2%)
    all_gather x1, waiting for transfers between devices, shards(): lax.all_gather(local_tokens, 'dp', axis=0, tiled=True)  50.6 us
    all_gather x1, blocking collectives, shards(): router_grad = jnp.sum(lax.all_gather(router_part, ('dp', 'expert')), axis=0)  44.9 us
    dot_general x3, matrix products, contract_cols(): lax.dot_general(left_side, right_side, (((1,), (1,)), ((), ())), preferre...  38 us
    dot_general x3, matrix products, contract_rows(): lax.dot_general(left_side, right_side, (((0,), (0,)), ((), ())), preferre...  36 us
    all_gather x1, waiting for transfers between devices, shards(): lax.all_gather(local_grads, 'dp', axis=0, tiled=True)  30.3 us
    psum x1, waiting for transfers between devices, shards(): lax.psum(grad_part.astype(jnp.bfloat16), 'tensor').astype(jnp.float32)  20 us
    reduce_scatter x1, waiting for transfers between devices, shards(): lax.psum_scatter(slot_dx.astype(jnp.bfloat16), 'dp', scatter_dimension=0,...  19.6 us
    unnamed x1, blocking collectives  12.1 us
  transfers between devices with their start and end apart: 6, of which 5 were waited for; matrix products, arithmetic and copies ran while one was open for 22% of the time, Pallas kernels for 0%

profile of v1, /device:TPU:0, one launch (start us, length us, event | category | flops | bytes accessed | tf_op | source)
XLA Modules:
  0.0 325.5 jit_solution(13892244223146294197)
XLA Ops:
  7.2 0.8 slice_bitcast_fusion.1
  8.0 0.8 compare_bitcast_fusion.1
  8.8 1.1 convolution_convert_fusion
  10.0 2.3 convolution_convert_fusion.1
  12.3 50.6 %all-gather.6.cloned.1.call-done = bf16[384,3072]{1,0:T(8,128)(2,1)} async-done(((bf16[96,3072]{1,0:T(8,128)(2,1)}), bf16[384,3072]{1,0:T(8,128)(2,1)}) %all-gather.6.cloned.1.call-update) | async-done | bytes 2359312 | tf_op jit(solution)/shard_map/all_gather | solution.py:85
  62.9 11.3 %fusion.31 = bf16[384,2048]{1,0:T(8,128)(2,1)} fusion(bf16[384,3072]{1,0:T(8,128)(2,1)} %all-gather.6.cloned.1.call-done, bf16[1,3072,2048]{2,1,0:T(8,128)(2,1)} %param.11), kind=kOutput, calls=%fused_computation.44 | convolution fusion | flops 4832624640 | bytes 16515072 | tf_op jit(solution)/shard_map/dot_general | solution.py:92
  74.1 9.4 %fusion.28 = bf16[384,2048]{1,0:T(8,128)(2,1)} fusion(bf16[384,3072]{1,0:T(8,128)(2,1)S(1)} %copy-done.8, bf16[1,3072,2048]{2,1,0:T(8,128)(2,1)} %param.12), kind=kOutput, calls=%fused_computation.43 | convolution fusion | flops 4832624640 | bytes 16515072 | tf_op jit(solution)/shard_map/dot_general | solution.py:93
  83.5 30.3 %all-gather.4.cloned.1.call-done = bf16[384,3072]{1,0:T(8,128)(2,1)} async-done(((bf16[96,3072]{1,0:T(8,128)(2,1)}), bf16[384,3072]{1,0:T(8,128)(2,1)}) %all-gather.4.cloned.1.call-update) | async-done | bytes 2359312 | tf_op jit(solution)/shard_map/all_gather | solution.py:86
  113.8 9.6 %fusion.25 = bf16[384,2048]{1,0:T(8,128)(2,1)} fusion(bf16[384,3072]{1,0:T(8,128)(2,1)} %all-gather.4.cloned.1.call-done, bf16[1,2048,3072]{2,1,0:T(8,128)(2,1)} %param.13), kind=kOutput, calls=%fused_computation.42 | convolution fusion | flops 4832624640 | bytes 16515072 | tf_op jit(solution)/shard_map/dot_general | solution.py:17
  123.5 0.6 copy-done.6
  124.4 0.3 fusion.66
  124.7 2.5 psum.28
  127.2 2.4 gather_fusion
  129.7 0.6 fusion.65
  131.5 20.0 %all-reduce.6.cloned.1.call-done = (bf16[384,2048]{1,0:T(8,128)(2,1)}, bf16[384,2048]{1,0:T(8,128)(2,1)}, bf16[384,2048]{1,0:T(8,128)(2,1)}) async-done(((bf16[384,2048]{1,0:T(8,128)(2,1)}, bf16[384,2048]{1,0:T(8,128)(2,1)}, bf16[384,2048]{1,0:T(8,128)(2,1)}), (bf16[384,2048]{1,0:T(8,128)(2,1)}, bf16[384,2048]{1,0:T(8,128)(2,1)}, bf16[384,2048]{1,0:T(8,128)(2,1)})) %all-reduce.6.cloned.1.call-update) | async-done | bytes 4718608 | tf_op jit(solution)/shard_map/psum | solution.py:98
  151.5 3.7 %fusion.14 = bf16[384]{0:T(512)(128)(2,1)S(1)} fusion(bf16[384,2048]{1,0:T(8,128)(2,1)} %get-tuple-element.7, bf16[384,2048]{1,0:T(8,128)(2,1)} %get-tuple-element.8, bf16[384,2048]{1,0:T(8,128)(2,1)} %get-tuple-element.9), kind=kLoop, calls=%fused_computation.31 | loop fusion | flops 9436800 | bytes 4719360 | tf_op jit(solution)/shard_map/reduce_sum | solution.py:49
  155.2 12.1 %all-reduce.2 = (bf16[384]{0:T(512)(128)(2,1)S(1)}, bf16[384]{0:T(512)(128)(2,1)S(1)}) all-reduce(bf16[384]{0:T(512)(128)(2,1)S(1)} %fusion.14, bf16[384]{0:T(512)(128)(2,1)S(1)} %dynamic-update-slice), channel_id=5, replica_groups=mesh['dp'=4,'expert'=4,'tensor'=2] {'dp'}, use_global_device_ids=true, to_apply=%region_7.8.clone | all-reduce | flops 768 | bytes 3072
  167.4 12.2 %fusion = f32[384,3072]{1,0:T(8,128)} fusion(bf16[1,3072,2048]{2,1,0:T(8,128)(2,1)} %param.11, bf16[384,2048]{1,0:T(8,128)(2,1)S(1)} %copy-done.1, bf16[384,2048]{1,0:T(8,128)(2,1)} %get-tuple-element.7, bf16[384,2048]{1,0:T(8,128)(2,1)} %get-tuple-element.9, f32[384]{0:T(512)S(1)} %convert_element_type.124), kind=kOutput, calls=%fused_computation.2 | convolution fusion | flops 4842848256 | bytes 22021632 | tf_op jit(solution)/shard_map/dot_general | solution.py:17
  179.6 16.1 %add_convert_fusion = bf16[384,3072]{1,0:T(8,128)(2,1)} fusion(f32[384,3072]{1,0:T(8,128)} %fusion, bf16[1,3072,2048]{2,1,0:T(8,128)(2,1)} %param.12, bf16[384,2048]{1,0:T(8,128)(2,1)S(1)} %copy-done.2, bf16[384,2048]{1,0:T(8,128)(2,1)} %get-tuple-element.7, f32[384]{0:T(512)S(1)} %convert_element_type.124), kind=kOutput, calls=%fused_computation.20 | convolution fusion | flops 4841275392 | bytes 22808064 | tf_op jit(solution)/shard_map/dot_general | solution.py:17
  197.2 0.7 copy.63
  198.3 13.5 %convert_bitcast_fusion.2 = bf16[1,3072,2048]{2,1,0:T(8,128)(2,1)} fusion(bf16[384,3072]{1,0:T(8,128)(2,1)} %all-gather.6.cloned.1.call-done, bf16[384,2048]{1,0:T(8,128)(2,1)S(1)} %copy-done.1, bf16[384,2048]{1,0:T(8,128)(2,1)} %get-tuple-element.7, bf16[384,2048]{1,0:T(8,128)(2,1)} %get-tuple-element.9, f32[384]{0:T(512)S(1)} %convert_element_type.124), kind=kOutput, calls=%fused_computation.14 | convolution fusion | flops 4849139712 | bytes 19662336 | tf_op jit(solution)/shard_map/dot_general | solution.py:11
  211.8 10.3 %convert_bitcast_fusion.1 = bf16[1,3072,2048]{2,1,0:T(8,128)(2,1)} fusion(bf16[384,3072]{1,0:T(8,128)(2,1)S(1)} %copy-done.9, bf16[384,2048]{1,0:T(8,128)(2,1)S(1)} %copy-done.3, bf16[384,2048]{1,0:T(8,128)(2,1)S(1)} %copy-done.4, f32[384]{0:T(512)S(1)} %convert_element_type.124), kind=kOutput, calls=%fused_computation.13 | convolution fusion | flops 4845207552 | bytes 18089472 | tf_op jit(solution)/shard_map/dot_general | solution.py:11
  222.1 19.6 %reduce-scatter.6.cloned.1.call-done = bf16[96,3072]{1,0:T(8,128)(2,1)} async-done(((bf16[384,3072]{1,0:T(8,128)(2,1)}), bf16[96,3072]{1,0:T(8,128)(2,1)}) %reduce-scatter.6.cloned.1.call-update) | async-done | bytes 589840 | tf_op jit(solution)/shard_map/reduce_scatter | solution.py:112
  241.8 1.5 fusion.48
  243.2 2.4 fusion.12
  245.6 12.1 %convert_bitcast_fusion = bf16[1,2048,3072]{2,1,0:T(8,128)(2,1)} fusion(bf16[384,3072]{1,0:T(8,128)(2,1)} %all-gather.4.cloned.1.call-done, f32[384]{0:T(512)S(1)} %convert_element_type.124, bf16[384,2048]{1,0:T(8,128)(2,1)S(1)} %copy-done.1, bf16[384,2048]{1,0:T(8,128)(2,1)} %get-tuple-element.9), kind=kOutput, calls=%fused_computation.12 | convolution fusion | flops 4847960064 | bytes 18089472 | tf_op jit(solution)/shard_map/dot_general | solution.py:11
  257.7 10.6 %reduce-scatter.10.cloned.1.call-done = bf16[32,4]{1,0:T(8,128)(2,1)} async-done(((bf16[128,4]{1,0:T(8,128)(2,1)}), bf16[32,4]{1,0:T(8,128)(2,1)}) %reduce-scatter.10.cloned.1.call-update) | async-done | bytes 272
  268.4 0.8 copy.64
  269.2 0.9 gather_fusion.1
  270.6 44.9 %all-gather = f32[49152,4]{0,1:T(4,128)S(1)} all-gather(f32[3072,4]{0,1:T(4,128)S(1)} %fusion.38), channel_id=2, replica_groups=mesh['dp'=4,'expert'=4,'tensor'=2] {'dp','expert'}, dimensions={0}, use_global_device_ids=true | all-gather | bytes 835584 | tf_op jit(solution)/shard_map/all_gather | solution.py:149
  315.5 1.1 bitcast_reduce_fusion
  316.6 2.0 fusion.13
  (60 shorter events, 2.9 us)
Async XLA Ops:
  7.2 1.6 copy-start
  7.2 55.7 %all-gather.6.cloned.1.call-start = ((), (), s32[]{:S(2)}) async-start(), calls=%async_computation.4 | async-start | bytes 2949120 | tf_op jit(solution)/shard_map/all_gather | solution.py:85
  9.9 103.9 %all-gather.4.cloned.1.call-start = ((), (), s32[]{:S(2)}) async-start(), calls=%async_computation.3 | async-start | bytes 2949120 | tf_op jit(solution)/shard_map/all_gather | solution.py:86
  12.3 139.3 %all-reduce.6.cloned.1.call-start = ((), (), s32[]{:S(2)}) async-start(), calls=%async_computation.8 | async-start | bytes 9437184 | tf_op jit(solution)/shard_map/psum | solution.py:98
  62.9 11.3 %copy-start.8 = (bf16[384,3072]{1,0:T(8,128)(2,1)S(1)}, bf16[384,3072]{1,0:T(8,128)(2,1)}, u32[]{:S(2)}) copy-start(bf16[384,3072]{1,0:T(8,128)(2,1)} %all-gather.6.cloned.1.call-done) | copy-start | bytes 7077892
  123.4 0.7 copy-start.6
  123.4 0.9 copy-start.5
  123.5 118.3 %reduce-scatter.6.cloned.1.call-start = ((), (), s32[]{:S(2)}) async-start(), calls=%async_computation.5 | async-start | bytes 2949120 | tf_op jit(solution)/shard_map/reduce_scatter | solution.py:112
  127.2 2.6 copy-start.7
  151.5 15.8 %copy-start.1 = (bf16[384,2048]{1,0:T(8,128)(2,1)S(1)}, bf16[384,2048]{1,0:T(8,128)(2,1)}, u32[]{:S(2)}) copy-start(bf16[384,2048]{1,0:T(8,128)(2,1)} %get-tuple-element.8) | copy-start | bytes 4718596
  167.4 12.2 %copy-start.2 = (bf16[384,2048]{1,0:T(8,128)(2,1)S(1)}, bf16[384,2048]{1,0:T(8,128)(2,1)}, u32[]{:S(2)}) copy-start(bf16[384,2048]{1,0:T(8,128)(2,1)} %get-tuple-element.9) | copy-start | bytes 4718596
  195.7 72.6 %reduce-scatter.10.cloned.1.call-start = ((), (), s32[]{:S(2)}) async-start(), calls=%async_computation.7 | async-start | bytes 40960
  198.0 118.7 %reduce-scatter.8.cloned.1.call-start = ((), (), s32[]{:S(2)}) async-start(), calls=%async_computation.6 | async-start | bytes 983040 | tf_op jit(solution)/shard_map/reduce_scatter | solution.py:122
  198.2 13.5 %copy-start.3 = (bf16[384,2048]{1,0:T(8,128)(2,1)S(1)}, bf16[384,2048]{1,0:T(8,128)(2,1)}, u32[]{:S(2)}) copy-start(bf16[384,2048]{1,0:T(8,128)(2,1)} %get-tuple-element.9) | copy-start | bytes 4718596
  198.3 13.5 %copy-start.4 = (bf16[384,2048]{1,0:T(8,128)(2,1)S(1)}, bf16[384,2048]{1,0:T(8,128)(2,1)}, u32[]{:S(2)}) copy-start(bf16[384,2048]{1,0:T(8,128)(2,1)} %get-tuple-element.7) | copy-start | bytes 4718596
  198.3 13.5 %copy-start.9 = (bf16[384,3072]{1,0:T(8,128)(2,1)S(1)}, bf16[384,3072]{1,0:T(8,128)(2,1)}, u32[]{:S(2)}) copy-start(bf16[384,3072]{1,0:T(8,128)(2,1)} %all-gather.6.cloned.1.call-done) | copy-start | bytes 7077892
Sparse Core Ops, SparseCore 0:
  10.1 52.6 all-gather.5
  65.0 48.7 all-gather.3
  123.6 27.9 all-reduce.5
  195.9 45.8 reduce-scatter.5
  244.9 23.4 reduce-scatter.9
  271.1 30.2 reduce-scatter.7
